TPU v7x, 8 devices: a whole 2x2x1 slice. The times are simulated.
8 devices in a mesh: data: 8 (over z, y, x, core).
Axes of the slice: x: 2, y: 2, z: 1, core: 2. Of those that a mesh axis runs over, the one named last changes fastest.
Arguments:
- x_tokens: bfloat16 [4096, 384], P('data')
- labels: int32 [3, 4096], P(None, 'data')
- w_up: bfloat16 [4, 384, 1536], replicated
- w_down: bfloat16 [4, 1536, 384], replicated
- task_heads: bfloat16 [3, 384, 13], replicated
Outputs:
- output 1: float32 [3], replicated
- output 2: float32 [3, 3], replicated
- output 3: float32 [4, 589824], P(None, 'data')
- output 4: float32 [4, 589824], P(None, 'data')
All inputs are finite; a program needn't handle non-finite values.
Results may differ from a plain program's by a relative error of at most 0.00354996.
Values are sent between devices in bfloat16 or wider.
A program may use at most 1 GiB of HBM per device.

v0:
```python
import jax
import jax.numpy as jnp
from jax import lax
from jax.sharding import PartitionSpec as P

EG_STEPS = 20


def simplex_weights(gram_mat):
    num_tasks = gram_mat.shape[0]
    value_a11 = jnp.trace(gram_mat) / num_tasks
    alpha_vec = jnp.full((num_tasks,), 1.0 / num_tasks, jnp.float32)
    for step_idx in range(EG_STEPS):
        grad_pull = jnp.sum(gram_mat * alpha_vec[None, :], axis=1)
        alpha_vec = alpha_vec * jnp.exp(-grad_pull / value_a11)
        alpha_vec = alpha_vec / jnp.sum(alpha_vec)
    return alpha_vec


def solution(mesh):
    num_dev = mesh.shape['data']

    def scatter_sum(part_grad, inv_tokens):
        num_tasks = part_grad.shape[0]
        flat_part = (part_grad.reshape(num_tasks, -1) * inv_tokens).astype(jnp.bfloat16)
        received = lax.all_to_all(flat_part, 'data', 1, 0, tiled=True)
        received = received.reshape(num_dev, num_tasks, -1)
        return jnp.sum(received, axis=0, dtype=jnp.float32)

    def local_step(x_local, lab_local, w_up, w_down, task_heads):
        num_layers = w_up.shape[0]
        num_classes = task_heads.shape[2]
        inv_tokens = 1.0 / (x_local.shape[0] * num_dev)
        hidden = x_local
        saved_acts = []
        for layer_idx in range(num_layers):
            pre_act = jnp.dot(hidden, w_up[layer_idx], preferred_element_type=jnp.float32)
            act_val, gelu_slope = jax.jvp(jax.nn.gelu, (pre_act,), (jnp.ones_like(pre_act),))
            act_bf = act_val.astype(jnp.bfloat16)
            mlp_out = jnp.dot(act_bf, w_down[layer_idx], preferred_element_type=jnp.float32)
            saved_acts.append((hidden, act_bf, gelu_slope))
            hidden = (hidden.astype(jnp.float32) + mlp_out).astype(jnp.bfloat16)
        logits = jnp.einsum('bd,tdc->tbc', hidden, task_heads, preferred_element_type=jnp.float32)
        soft_probs = jax.nn.softmax(logits, axis=-1)
        onehot = (lab_local[:, :, None] == jnp.arange(num_classes)[None, None, :]).astype(jnp.float32)
        head_err = (soft_probs - onehot).astype(jnp.bfloat16)
        d_hidden = jnp.einsum('tbc,tdc->tbd', head_err, task_heads, preferred_element_type=jnp.float32).astype(jnp.bfloat16)
        up_shards = [None] * num_layers
        down_shards = [None] * num_layers
        for layer_idx in range(num_layers - 1, -1, -1):
            hidden_in, act_bf, gelu_slope = saved_acts[layer_idx]
            down_grad = jnp.einsum('bf,tbd->tfd', act_bf, d_hidden, preferred_element_type=jnp.float32)
            down_shards[layer_idx] = scatter_sum(down_grad, inv_tokens)
            d_act = jnp.einsum('tbd,fd->tbf', d_hidden, w_down[layer_idx], preferred_element_type=jnp.float32)
            d_pre = (d_act * gelu_slope[None]).astype(jnp.bfloat16)
            up_grad = jnp.einsum('bd,tbf->tdf', hidden_in, d_pre, preferred_element_type=jnp.float32)
            up_shards[layer_idx] = scatter_sum(up_grad, inv_tokens)
            if layer_idx > 0:
                d_hidden = (d_hidden.astype(jnp.float32) + jnp.einsum('tbf,df->tbd', d_pre, w_up[layer_idx], preferred_element_type=jnp.float32)).astype(jnp.bfloat16)
        gram_part = sum(jnp.einsum('ts,us->tu', grad_shard, grad_shard, precision=lax.Precision.HIGHEST, preferred_element_type=jnp.float32) for grad_shard in up_shards + down_shards)
        gram_mat = lax.psum(gram_part, 'data')
        task_weights = simplex_weights(gram_mat)
        grad_up = jnp.stack([jnp.sum(task_weights[:, None] * grad_shard, axis=0) for grad_shard in up_shards])
        grad_down = jnp.stack([jnp.sum(task_weights[:, None] * grad_shard, axis=0) for grad_shard in down_shards])
        return task_weights, gram_mat, grad_up, grad_down

    return jax.shard_map(local_step, mesh=mesh, in_specs=(P('data', None), P(None, 'data'), P(), P(), P()), out_specs=(P(), P(), P(None, 'data'), P(None, 'data')), check_vma=False)
```

profile of v0, /device:TPU:0, one launch (start us, length us, event | category | flops | bytes accessed | tf_op | source)
XLA Modules:
  0.0 616.8 jit_solution(17808680727960796891)
XLA Ops:
  43.6 6.0 copy.76
  55.1 7.2 %copy.77 = bf16[3,8,73728]{2,0,1:T(4,128)(2,1)} copy(bf16[3,8,73728]{2,1,0:T(8,128)(2,1)} %convert_element_type.238) | data formatting | bytes 7077888 | tf_op jit(solution)/shard_map/convert_element_type | solution.py:25
  66.9 6.9 %fusion.4 = bf16[3,384,1536]{1,2,0:T(8,128)(2,1)} fusion(bf16[3,512,1536]{2,1,0:T(8,128)(2,1)} %copy-done.9, bf16[512,384]{1,0:T(8,128)(2,1)} %copy-done.24), kind=kOutput, calls=%fused_computation.32 | convolution fusion | flops 1815478272 | bytes 8650752 | tf_op jit(solution)/shard_map/bd,tbf->tdf/dot_general | solution.py:56
  73.7 6.1 copy.67
  85.3 7.3 %copy.68 = bf16[3,8,73728]{2,0,1:T(4,128)(2,1)} copy(bf16[3,8,73728]{2,1,0:T(8,128)(2,1)} %convert_element_type.226) | data formatting | bytes 7077888 | tf_op jit(solution)/shard_map/convert_element_type | solution.py:25
  92.6 28.9 %all-to-all-done.6 = bf16[3,8,73728]{2,0,1:T(4,128)(2,1)} async-done(((bf16[3,8,73728]{2,0,1:T(4,128)(2,1)}), bf16[3,8,73728]{2,0,1:T(4,128)(2,1)}, u32[]{:S(2)}, u32[]{:S(2)}) %all-to-all-start.6) | async-done | bytes 3538976 | tf_op jit(solution)/shard_map/all_to_all | solution.py:26
  129.9 6.0 add_convert_fusion.1
  139.9 6.0 copy.73
  151.5 7.3 %copy.74 = bf16[3,8,73728]{2,0,1:T(4,128)(2,1)} copy(bf16[3,8,73728]{2,1,0:T(8,128)(2,1)} %convert_element_type.234) | data formatting | bytes 7077888 | tf_op jit(solution)/shard_map/convert_element_type | solution.py:25
  158.8 21.0 %all-to-all-done.3 = bf16[3,8,73728]{2,0,1:T(4,128)(2,1)} async-done(((bf16[3,8,73728]{2,0,1:T(4,128)(2,1)}), bf16[3,8,73728]{2,0,1:T(4,128)(2,1)}, u32[]{:S(2)}, u32[]{:S(2)}) %all-to-all-start.3) | async-done | bytes 3538976 | tf_op jit(solution)/shard_map/all_to_all | solution.py:26
  183.6 6.9 %fusion.3 = bf16[3,384,1536]{1,2,0:T(8,128)(2,1)} fusion(bf16[3,512,1536]{2,1,0:T(8,128)(2,1)} %copy-done.8, bf16[512,384]{1,0:T(8,128)(2,1)} %copy-done.23), kind=kOutput, calls=%fused_computation.31 | convolution fusion | flops 1815478272 | bytes 8650752 | tf_op jit(solution)/shard_map/bd,tbf->tdf/dot_general | solution.py:56
  190.4 6.1 copy.64
  202.1 7.2 %copy.65 = bf16[3,8,73728]{2,0,1:T(4,128)(2,1)} copy(bf16[3,8,73728]{2,1,0:T(8,128)(2,1)} %convert_element_type.222) | data formatting | bytes 7077888 | tf_op jit(solution)/shard_map/convert_element_type | solution.py:25
  209.3 28.9 %all-to-all-done.5 = bf16[3,8,73728]{2,0,1:T(4,128)(2,1)} async-done(((bf16[3,8,73728]{2,0,1:T(4,128)(2,1)}), bf16[3,8,73728]{2,0,1:T(4,128)(2,1)}, u32[]{:S(2)}, u32[]{:S(2)}) %all-to-all-start.5) | async-done | bytes 3538976 | tf_op jit(solution)/shard_map/all_to_all | solution.py:26
  252.2 10.2 %fusion.1 = bf16[3,384,1536]{1,2,0:T(8,128)(2,1)} fusion(bf16[3,512,384]{2,1,0:T(8,128)(2,1)} %add_convert_fusion, f32[512,1536]{1,0:T(8,128)} %get-tuple-element.60, bf16[4,1536,384]{2,1,0:T(8,128)(2,1)} %param.8, bf16[512,384]{1,0:T(8,128)(2,1)S(1)} %copy-done.16), kind=kOutput, calls=%fused_computation.29 | convolution fusion | flops 3632136192 | bytes 9437184 | tf_op jit(solution)/shard_map/bd,tbf->tdf/dot_general | solution.py:56
  262.4 6.1 copy.58
  273.9 7.3 %copy.59 = bf16[3,8,73728]{2,0,1:T(4,128)(2,1)} copy(bf16[3,8,73728]{2,1,0:T(8,128)(2,1)} %convert_element_type.214) | data formatting | bytes 7077888 | tf_op jit(solution)/shard_map/convert_element_type | solution.py:25
  281.2 15.1 %all-to-all-done.2 = bf16[3,8,73728]{2,0,1:T(4,128)(2,1)} async-done(((bf16[3,8,73728]{2,0,1:T(4,128)(2,1)}), bf16[3,8,73728]{2,0,1:T(4,128)(2,1)}, u32[]{:S(2)}, u32[]{:S(2)}) %all-to-all-start.2) | async-done | bytes 3538976 | tf_op jit(solution)/shard_map/all_to_all | solution.py:26
  299.9 6.8 %fusion.2 = bf16[3,384,1536]{1,2,0:T(8,128)(2,1)} fusion(bf16[3,512,1536]{2,1,0:T(8,128)(2,1)} %copy-done.7, bf16[512,384]{1,0:T(8,128)(2,1)S(1)} %fusion.53), kind=kOutput, calls=%fused_computation.30 | convolution fusion | flops 1815478272 | bytes 8650752 | tf_op jit(solution)/shard_map/bd,tbf->tdf/dot_general | solution.py:56
  306.6 6.1 copy.61
  318.2 7.2 %copy.62 = bf16[3,8,73728]{2,0,1:T(4,128)(2,1)} copy(bf16[3,8,73728]{2,1,0:T(8,128)(2,1)} %convert_element_type.218) | data formatting | bytes 7077888 | tf_op jit(solution)/shard_map/convert_element_type | solution.py:25
  325.4 29.1 %all-to-all-done = bf16[3,8,73728]{2,0,1:T(4,128)(2,1)} async-done(((bf16[3,8,73728]{2,0,1:T(4,128)(2,1)}), bf16[3,8,73728]{2,0,1:T(4,128)(2,1)}, u32[]{:S(2)}, u32[]{:S(2)}) %all-to-all-start) | async-done | bytes 3538976 | tf_op jit(solution)/shard_map/all_to_all | solution.py:26
  358.3 5.9 fusion.5
  364.1 6.0 copy.70
  375.7 7.2 %copy.71 = bf16[3,8,73728]{2,0,1:T(4,128)(2,1)} copy(bf16[3,8,73728]{2,1,0:T(8,128)(2,1)} %convert_element_type.230) | data formatting | bytes 7077888 | tf_op jit(solution)/shard_map/convert_element_type | solution.py:25
  382.9 30.0 %all-to-all-done.1 = bf16[3,8,73728]{2,0,1:T(4,128)(2,1)} async-done(((bf16[3,8,73728]{2,0,1:T(4,128)(2,1)}), bf16[3,8,73728]{2,0,1:T(4,128)(2,1)}, u32[]{:S(2)}, u32[]{:S(2)}) %all-to-all-start.1) | async-done | bytes 3538976 | tf_op jit(solution)/shard_map/all_to_all | solution.py:26
  422.1 6.0 copy.79
  433.8 7.2 %copy.80 = bf16[3,8,73728]{2,0,1:T(4,128)(2,1)} copy(bf16[3,8,73728]{2,1,0:T(8,128)(2,1)} %convert_element_type.242) | data formatting | bytes 7077888 | tf_op jit(solution)/shard_map/convert_element_type | solution.py:25
  474.2 7.1 %convolution_add_fusion.9 = f32[3,3]{1,0:T(4,128)S(1)} fusion(f32[3,3]{1,0:T(4,128)S(1)} %convolution_add_fusion.10, f32[3,73728]{1,0:T(4,128)} %convert_reduce_fusion.5), kind=kOutput, calls=%fused_computation.137 | convolution fusion | flops 7962633 | bytes 884808 | tf_op jit(solution)/shard_map/ts,us->tu/dot_general | solution.py:60
  522.5 6.3 %all-to-all-done.7 = bf16[3,8,73728]{2,0,1:T(4,128)(2,1)} async-done(((bf16[3,8,73728]{2,0,1:T(4,128)(2,1)}), bf16[3,8,73728]{2,0,1:T(4,128)(2,1)}, u32[]{:S(2)}, u32[]{:S(2)}) %all-to-all-start.7) | async-done | bytes 3538976 | tf_op jit(solution)/shard_map/all_to_all | solution.py:26
  539.8 22.5 %psum.7 = f32[3,3]{1,0:T(4,128)S(1)} all-reduce(f32[3,3]{1,0:T(4,128)S(1)} %convolution_add_fusion.4), channel_id=1, replica_groups=mesh['data'=8] {'data'}, use_global_device_ids=true, to_apply=%region_10.0 | all-reduce | flops 9 | bytes 72 | tf_op jit(solution)/shard_map/psum | solution.py:61
  601.8 11.4 %multiply_reduce_fusion.3 = (f32[73728]{0:T(1024)S(1)}, f32[73728]{0:T(1024)S(1)}, f32[73728]{0:T(1024)S(1)}, f32[73728]{0:T(1024)S(1)}, f32[73728]{0:T(1024)S(1...) fusion(f32[3,73728]{1,0:T(4,128)} %copy-done.3, f32[3]{0:T(128)S(1)} %broadcast_divide_fusion, ...), kind=kLoop, calls=%fused_computation.122 | loop fusion | flops 2949120 | bytes 9437196 | tf_op jit(solution)/shard_map/reduce_sum | solution.py:64
  (161 shorter events, 265.4 us)
Async XLA Ops:
  0.6 24.8 %copy-start = (bf16[3,384,13]{1,2,0:T(8,128)(2,1)S(1)}, bf16[3,384,13]{1,2,0:T(8,128)(2,1)}, u32[]{:S(2)}) copy-start(bf16[3,384,13]{1,2,0:T(8,128)(2,1)} %param.9) | copy-start | bytes 89860
  0.6 5.4 copy-start.16
  0.7 5.4 copy-start.10
  6.0 1.7 copy-start.17
  6.0 3.5 copy-start.15
  13.3 1.7 copy-start.18
  15.0 3.9 copy-start.23
  18.9 1.7 copy-start.20
  20.7 4.7 copy-start.24
  25.4 3.9 copy-start.13
  34.5 5.0 copy-start.9
  34.5 5.0 copy-start.21
  39.5 85.6 %copy-start.11 = (bf16[3,512,384]{2,1,0:T(8,128)(2,1)}, bf16[3,512,384]{2,1,0:T(8,128)(2,1)S(1)}, u32[]{:S(2)}) copy-start(bf16[3,512,384]{2,1,0:T(8,128)(2,1)S(1)} %add_convert_fusion.2) | copy-start | bytes 3538948
  62.3 59.2 %all-to-all-start.6 = ((bf16[3,8,73728]{2,0,1:T(4,128)(2,1)}), bf16[3,8,73728]{2,0,1:T(4,128)(2,1)}, u32[]{:S(2)}, u32[]{:S(2)}) async-start(bf16[3,8,73728]{2,0,1:T(4,128)(2,1)} %copy.77), calls=%async_computation.6 | async-start | bytes 9437184 | tf_op jit(solution)/shard_map/all_to_all | solution.py:26
  121.5 58.2 %all-to-all-start.3 = ((bf16[3,8,73728]{2,0,1:T(4,128)(2,1)}), bf16[3,8,73728]{2,0,1:T(4,128)(2,1)}, u32[]{:S(2)}, u32[]{:S(2)}) async-start(bf16[3,8,73728]{2,0,1:T(4,128)(2,1)} %copy.68), calls=%async_computation.3 | async-start | bytes 9437184 | tf_op jit(solution)/shard_map/all_to_all | solution.py:26
  129.8 6.0 copy-start.8
  129.8 6.0 copy-start.19
  179.8 58.4 %all-to-all-start.5 = ((bf16[3,8,73728]{2,0,1:T(4,128)(2,1)}), bf16[3,8,73728]{2,0,1:T(4,128)(2,1)}, u32[]{:S(2)}, u32[]{:S(2)}) async-start(bf16[3,8,73728]{2,0,1:T(4,128)(2,1)} %copy.74), calls=%async_computation.5 | async-start | bytes 9437184 | tf_op jit(solution)/shard_map/all_to_all | solution.py:26
  238.2 58.1 %all-to-all-start.2 = ((bf16[3,8,73728]{2,0,1:T(4,128)(2,1)}), bf16[3,8,73728]{2,0,1:T(4,128)(2,1)}, u32[]{:S(2)}, u32[]{:S(2)}) async-start(bf16[3,8,73728]{2,0,1:T(4,128)(2,1)} %copy.65), calls=%async_computation.2 | async-start | bytes 9437184 | tf_op jit(solution)/shard_map/all_to_all | solution.py:26
  246.4 5.9 copy-start.7
  296.3 58.2 %all-to-all-start = ((bf16[3,8,73728]{2,0,1:T(4,128)(2,1)}), bf16[3,8,73728]{2,0,1:T(4,128)(2,1)}, u32[]{:S(2)}, u32[]{:S(2)}) async-start(bf16[3,8,73728]{2,0,1:T(4,128)(2,1)} %copy.59), calls=%async_computation | async-start | bytes 9437184 | tf_op jit(solution)/shard_map/all_to_all | solution.py:26
  325.4 32.9 %copy-start.22 = (bf16[3,512,384]{2,1,0:T(8,128)(2,1)S(1)}, bf16[3,512,384]{2,1,0:T(8,128)(2,1)}, u32[]{:S(2)}) copy-start(bf16[3,512,384]{2,1,0:T(8,128)(2,1)} %add_convert_fusion) | copy-start | bytes 3538948
  354.5 58.4 %all-to-all-start.1 = ((bf16[3,8,73728]{2,0,1:T(4,128)(2,1)}), bf16[3,8,73728]{2,0,1:T(4,128)(2,1)}, u32[]{:S(2)}, u32[]{:S(2)}) async-start(bf16[3,8,73728]{2,0,1:T(4,128)(2,1)} %copy.62), calls=%async_computation.1 | async-start | bytes 9437184 | tf_op jit(solution)/shard_map/all_to_all | solution.py:26
  412.9 57.9 %all-to-all-start.4 = ((bf16[3,8,73728]{2,0,1:T(4,128)(2,1)}), bf16[3,8,73728]{2,0,1:T(4,128)(2,1)}, u32[]{:S(2)}, u32[]{:S(2)}) async-start(bf16[3,8,73728]{2,0,1:T(4,128)(2,1)} %copy.71), calls=%async_computation.4 | async-start | bytes 9437184 | tf_op jit(solution)/shard_map/all_to_all | solution.py:26
  470.8 58.0 %all-to-all-start.7 = ((bf16[3,8,73728]{2,0,1:T(4,128)(2,1)}), bf16[3,8,73728]{2,0,1:T(4,128)(2,1)}, u32[]{:S(2)}, u32[]{:S(2)}) async-start(bf16[3,8,73728]{2,0,1:T(4,128)(2,1)} %copy.80), calls=%async_computation.7 | async-start | bytes 9437184 | tf_op jit(solution)/shard_map/all_to_all | solution.py:26
  485.9 10.1 %copy-start.2 = (f32[3,73728]{1,0:T(4,128)}, f32[3,73728]{1,0:T(4,128)S(1)}, u32[]{:S(2)}) copy-start(f32[3,73728]{1,0:T(4,128)S(1)} %convert_reduce_fusion.4) | copy-start | bytes 2654212
  496.0 10.0 %copy-start.3 = (f32[3,73728]{1,0:T(4,128)}, f32[3,73728]{1,0:T(4,128)S(1)}, u32[]{:S(2)}) copy-start(f32[3,73728]{1,0:T(4,128)S(1)} %convert_reduce_fusion.3) | copy-start | bytes 2654212
  506.0 10.0 %copy-start.4 = (f32[3,73728]{1,0:T(4,128)}, f32[3,73728]{1,0:T(4,128)S(1)}, u32[]{:S(2)}) copy-start(f32[3,73728]{1,0:T(4,128)S(1)} %convert_reduce_fusion.2) | copy-start | bytes 2654212
  533.5 1.1 copy-start.6
  562.3 50.8 %copy-start.12 = (f32[3,3]{1,0:T(4,128)}, f32[3,3]{1,0:T(4,128)S(1)}, u32[]{:S(2)}) copy-start(f32[3,3]{1,0:T(4,128)S(1)} %psum.7) | copy-start | bytes 112
  601.7 11.4 %copy-start.14 = (f32[3]{0:T(128)}, f32[3]{0:T(128)S(1)}, u32[]{:S(2)}) copy-start(f32[3]{0:T(128)S(1)} %broadcast_divide_fusion) | copy-start | bytes 40
  601.8 14.6 %copy-start.1 = (bf16[3,384,13]{1,2,0:T(8,128)(2,1)S(1)}, bf16[3,384,13]{1,2,0:T(8,128)(2,1)}, u32[]{:S(2)}) copy-start(bf16[3,384,13]{1,2,0:T(8,128)(2,1)} %param.9) | copy-start | bytes 89860
  (1 other events, 1.0 us)
where the time goes:
time: 629 us; the launch traced here: 617 us
  waiting for transfers between devices  163 us (26%)
  local copies, waits for them, and re-layouts  156 us (25%)
  matrix products  152 us (24%)
  other arithmetic  91.8 us (15%)
  starting transfers between devices  29.4 us (5%)
  blocking collectives  22.5 us (4%)
    all_to_all x8, waiting for transfers between devices, scatter_sum(): received = lax.all_to_all(flat_part, 'data', 1, 0, tiled=True)  163 us
    convert_element_type x24, local copies, waits for them, and re-layouts, scatter_sum(): (part_grad.reshape(num_tasks, -1) * inv_tokens).astype(jnp.bfloat16)  150 us
    dot_general x8, matrix products, local_step(): jnp.einsum('ts,us->tu', grad_shard, grad_shard, precision=lax.Precision.H...  44.7 us
    reduce_sum x8, other arithmetic, scatter_sum(): return jnp.sum(received, axis=0, dtype=jnp.float32)  38.5 us
    dot_general x4, matrix products, local_step(): jnp.einsum('bd,tbf->tdf', hidden_in, d_pre, preferred_element_type=jnp.fl...  30.7 us
    all_to_all x8, starting transfers between devices, scatter_sum(): received = lax.all_to_all(flat_part, 'data', 1, 0, tiled=True)  29.4 us
    reduce_sum x20, other arithmetic, simplex_weights(): alpha_vec = alpha_vec / jnp.sum(alpha_vec)  23.7 us
    psum x1, blocking collectives, local_step(): gram_mat = lax.psum(gram_part, 'data')  22.5 us
  transfers between devices with their start and end apart: 8, of which 8 were waited for; matrix products, arithmetic and copies ran while one was open for 44% of the time, Pallas kernels for 0%

commit v1 on v0

v1 whole, which is shorter than its diff:
```python
import math

import jax
import jax.numpy as jnp
from jax import lax
from jax.experimental import pallas as pl
from jax.experimental.pallas import tpu as pltpu
from jax.sharding import PartitionSpec as P

EG_STEPS = 20
MESH = pl.DeviceIdType.MESH
GELU_C = math.sqrt(2.0 / math.pi)
GELU_A = 0.044715
F32 = jnp.float32
BF16 = jnp.bfloat16
PAIRS = ((0, 0), (0, 1), (0, 2), (1, 1), (1, 2), (2, 2))
CORES = 2
CHIPS = 4


def dot_nn(lhs, rhs):
    return lax.dot_general(lhs, rhs, (((1,), (0,)), ((), ())), preferred_element_type=F32)


def dot_nt(lhs, rhs):
    return lax.dot_general(lhs, rhs, (((1,), (1,)), ((), ())), preferred_element_type=F32)


def dot_tn(lhs, rhs):
    return lax.dot_general(lhs, rhs, (((0,), (0,)), ((), ())), preferred_element_type=F32)


def dot_tt(lhs, rhs):
    return lax.dot_general(lhs, rhs, (((0,), (1,)), ((), ())), preferred_element_type=F32)


def gelu_act(pre):
    tanh_val = jnp.tanh(pre * (GELU_C + (GELU_C * GELU_A) * (pre * pre)))
    return pre * (0.5 * tanh_val + 0.5)


def gelu_slope(pre):
    sq_pre = pre * pre
    tanh_val = jnp.tanh(pre * (GELU_C + (GELU_C * GELU_A) * sq_pre))
    rise = pre * (0.5 * GELU_C + (1.5 * GELU_C * GELU_A) * sq_pre)
    return (0.5 * tanh_val + 0.5) + rise * (1.0 - tanh_val * tanh_val)


def trunk_kernel(inv_tokens, x_ref, lab_ref, w1_hbm, w2_hbm, head_ref, stat_ref, outu_ref, outd_ref,
                 w1, w2, xg, lg, hs, pre, act, akeep, dstack, dcat, sbuf, scat, accu, accd, recvu, recvd,
                 gsend, grecv, mtile, w_sem, xs_sem, xr_sem, ls_sem, lr_sem, us_sem, ur_sem, ds_sem, dr_sem,
                 ms_sem, mr_sem, gs_sem, gr_sem):
    num_layers, num_tasks = w1.shape[0], head_ref.shape[0]
    tok, dim = x_ref.shape
    ff = w1.shape[2]
    ffq = ff // CHIPS
    num_dev = CORES * CHIPS
    me = lax.axis_index('data')
    chip, core = me // CORES, me % CORES
    mate = me + 1 - 2 * core
    mcore = 1 - core
    cx, cy = chip % 2, chip // 2
    peer_chip = (cy * 2 + (1 - cx), (1 - cy) * 2 + cx, (1 - cy) * 2 + (1 - cx))
    peers = tuple(pc * CORES + core for pc in peer_chip)

    w_copies = []
    for layer in range(num_layers):
        c1 = pltpu.make_async_copy(w1_hbm.at[layer], w1.at[layer], w_sem.at[0, layer])
        c2 = pltpu.make_async_copy(w2_hbm.at[layer], w2.at[layer], w_sem.at[1, layer])
        c1.start()
        c2.start()
        w_copies.append((c1, c2))

    barrier = pltpu.get_barrier_semaphore()
    for step in range(1, num_dev):
        pl.semaphore_signal(barrier, inc=1, device_id=(lax.rem(me + step, num_dev),), device_id_type=MESH)
    pl.semaphore_wait(barrier, num_dev - 1)

    x_copies, l_copies = [], []
    for slot in range(3):
        x_copies.append(pltpu.make_async_remote_copy(
            src_ref=x_ref, dst_ref=xg.at[slot], send_sem=xs_sem.at[slot], recv_sem=xr_sem.at[slot],
            device_id=(peers[slot],), device_id_type=MESH))
        l_copies.append(pltpu.make_async_remote_copy(
            src_ref=lab_ref, dst_ref=lg.at[slot], send_sem=ls_sem.at[slot], recv_sem=lr_sem.at[slot],
            device_id=(peers[slot],), device_id_type=MESH))
    for slot in range(3):
        x_copies[slot].start()
        l_copies[slot].start()

    fk = pl.ds(pl.multiple_of(chip * ffq, 128), ffq)

    def forward(layer):
        h_in = hs[layer]

        @pl.loop(0, 3)
        def _(blk):
            cols = pl.ds(pl.multiple_of(blk * 512, 512), 512)
            p_val = dot_nn(h_in, w1[layer, :, cols])
            pre[layer, :, cols] = p_val
            act[:, cols] = gelu_act(p_val).astype(BF16)

        akeep[layer] = act[:, fk]
        hs[layer + 1] = (h_in.astype(F32) + dot_nn(act[...], w2[layer])).astype(BF16)

    def weight_grads(layer, first):
        down = dot_tn(akeep[layer], dcat[...])
        up = dot_tn(hs[layer], scat[...])
        for task in range(num_tasks):
            d_new = down[:, task * dim:(task + 1) * dim].reshape(2, ffq // 2, dim)
            u_new = up[:, task * ffq:(task + 1) * ffq].reshape(CHIPS, CORES, dim // 8, ffq)

            if first:
                accd[layer, task] = d_new
                accu[layer, task] = u_new
            else:
                accd[layer, task] += d_new
                accu[layer, task] += u_new

    def backward_full(layer, first):
        @pl.loop(0, 3)
        def _(blk):
            cols = pl.ds(pl.multiple_of(blk * 512, 512), 512)
            slope = gelu_slope(pre[layer, :, cols])
            w_blk = w2[layer, cols, :]
            for task in range(num_tasks):
                d_act = dot_nt(dstack[task], w_blk)
                sbuf[task, :, cols] = (d_act * slope).astype(BF16)

        for task in range(num_tasks):
            scat[:, task * ffq:(task + 1) * ffq] = sbuf[task, :, fk]
        weight_grads(layer, first)
        for task in range(num_tasks):
            d_new = dstack[task].astype(F32) + dot_nt(sbuf[task], w1[layer])
            d_new = d_new.astype(BF16)
            dstack[task] = d_new
            dcat[:, task * dim:(task + 1) * dim] = d_new

    def backward_first(first):
        slope = gelu_slope(pre[0, :, fk])
        for task in range(num_tasks):
            d_act = dot_nt(dstack[task], w2[0, fk, :])
            scat[:, task * ffq:(task + 1) * ffq] = (d_act * slope).astype(BF16)
        weight_grads(0, first)

    def head_errors(labels):
        z_val = hs[num_layers]
        for task in range(num_tasks):
            logits = dot_tt(head_ref[task], z_val)
            shifted = jnp.exp(logits - jnp.max(logits, axis=0, keepdims=True))
            probs = shifted / jnp.sum(shifted, axis=0, keepdims=True)
            rows = lax.broadcasted_iota(jnp.int32, probs.shape, 0)
            onehot = (rows == labels[task:task + 1, :]).astype(F32)
            err = (probs - onehot).astype(BF16)
            d_val = dot_tt(err, head_ref[task]).astype(BF16)
            dstack[task] = d_val
            dcat[:, task * dim:(task + 1) * dim] = d_val

    u_copies, d_copies = [], []
    for layer in range(num_layers):
        u_copies.append(pltpu.make_async_remote_copy(
            src_ref=accu.at[layer, :, :, mcore], dst_ref=recvu.at[layer], send_sem=us_sem.at[layer],
            recv_sem=ur_sem.at[layer], device_id=(mate,), device_id_type=MESH))
        d_copies.append(pltpu.make_async_remote_copy(
            src_ref=accd.at[layer, :, mcore], dst_ref=recvd.at[layer], send_sem=ds_sem.at[layer],
            recv_sem=dr_sem.at[layer], device_id=(mate,), device_id_type=MESH))

    def zero_acc(layer):
        accu[layer] = jnp.zeros(accu.shape[1:], F32)
        accd[layer] = jnp.zeros(accd.shape[1:], F32)

    @pl.loop(0, num_layers)
    def _(layer):
        zero_acc(layer)

    @pl.loop(0, CHIPS)
    def _(quarter):
        @pl.when(quarter == 0)
        def _():
            hs[0] = x_ref[...]

        for slot in range(3):
            @pl.when(quarter == slot + 1)
            def _():
                x_copies[slot].wait_recv()
                l_copies[slot].wait_recv()
                hs[0] = xg[slot]

        for layer in range(num_layers):
            @pl.when(quarter == 0)
            def _():
                w_copies[layer][0].wait()
                w_copies[layer][1].wait()

        @pl.loop(0, num_layers)
        def _(layer):
            forward(layer)

        @pl.when(quarter == 0)
        def _():
            head_errors(lab_ref[...])

        @pl.when(quarter > 0)
        def _():
            head_errors(lg[jnp.maximum(quarter - 1, 0)])

        @pl.loop(0, num_layers - 1)
        def _(back):
            layer = num_layers - 1 - back
            backward_full(layer, False)
            for sent in range(1, num_layers):
                @pl.when(jnp.logical_and(quarter == CHIPS - 1, layer == sent))
                def _():
                    u_copies[sent].start()
                    d_copies[sent].start()

        backward_first(False)

    u_copies[0].start()
    d_copies[0].start()
    for slot in range(3):
        x_copies[slot].wait_send()
        l_copies[slot].wait_send()

    sums = tuple(jnp.zeros((8, 128), F32) for _ in PAIRS)

    def fold(val):
        tiles = val.reshape(-1, 8, val.shape[-1])
        part = jnp.sum(tiles, axis=0)
        out = part[:, :128]
        for piece in range(1, part.shape[-1] // 128):
            out = out + part[:, piece * 128:(piece + 1) * 128]
        return out

    def gram(sums, grads):
        return tuple(acc + fold(grads[t] * grads[s]) for acc, (t, s) in zip(sums, PAIRS))

    for layer in range(num_layers - 1, -1, -1):
        u_copies[layer].wait_recv()
        d_copies[layer].wait_recv()

        @pl.loop(0, CHIPS, init_carry=sums)
        def sums(block, carry):
            grads = []
            for task in range(num_tasks):
                val = (accu[layer, task, block, core] + recvu[layer, task, block]) * inv_tokens
                recvu[layer, task, block] = val
                grads.append(val)
            return gram(carry, grads)

        @pl.loop(0, 4, init_carry=sums)
        def sums(block, carry):
            rows = pl.ds(pl.multiple_of(block * 48, 48), 48)
            grads = []
            for task in range(num_tasks):
                val = (accd[layer, task, core, rows] + recvd[layer, task, rows]) * inv_tokens
                recvd[layer, task, rows] = val
                grads.append(val)
            return gram(carry, grads)

    tile_rows = lax.broadcasted_iota(jnp.int32, (8, 128), 0)
    my_tile = jnp.zeros((8, 128), F32)
    for row, acc in enumerate(sums):
        my_tile = jnp.where(tile_rows == row, jnp.sum(acc, axis=0, keepdims=True), my_tile)
    mtile[me] = my_tile
    m_copies = []
    for step in range(1, num_dev):
        m_copies.append(pltpu.make_async_remote_copy(
            src_ref=mtile.at[me], dst_ref=mtile.at[me], send_sem=ms_sem.at[step - 1], recv_sem=mr_sem.at[step - 1],
            device_id=(lax.rem(me + step, num_dev),), device_id_type=MESH))
    for copy in m_copies:
        copy.start()
    for layer in range(num_layers):
        u_copies[layer].wait_send()
        d_copies[layer].wait_send()
    for step in range(1, num_dev):
        src_dev = lax.rem(me + num_dev - step, num_dev)
        pltpu.make_async_remote_copy(
            src_ref=mtile.at[src_dev], dst_ref=mtile.at[src_dev], send_sem=ms_sem.at[step - 1],
            recv_sem=mr_sem.at[step - 1], device_id=(lax.rem(me + step, num_dev),), device_id_type=MESH).wait_recv()
    total = mtile[0]
    for dev in range(1, num_dev):
        total = total + mtile[dev]
    total = jnp.broadcast_to(jnp.sum(total, axis=1, keepdims=True), (8, 128))
    entry = {}
    for row, (t, s) in enumerate(PAIRS):
        val = jnp.broadcast_to(total[row:row + 1, :], (8, 128))
        entry[t, s] = val
        entry[s, t] = val
    tau = (entry[0, 0] + entry[1, 1] + entry[2, 2]) / num_tasks
    alpha = [jnp.full((8, 128), 1.0 / num_tasks, F32) for _ in range(num_tasks)]
    for step in range(EG_STEPS):
        pulls = [entry[t, 0] * alpha[0] + entry[t, 1] * alpha[1] + entry[t, 2] * alpha[2] for t in range(num_tasks)]
        alpha = [alpha[t] * jnp.exp(-pulls[t] / tau) for t in range(num_tasks)]
        norm = alpha[0] + alpha[1] + alpha[2]
        alpha = [a / norm for a in alpha]
    lanes = lax.broadcasted_iota(jnp.int32, (8, 128), 1)
    stat = jnp.zeros((8, 128), F32)
    for t in range(num_tasks):
        stat = jnp.where(jnp.logical_and(tile_rows == 0, lanes == t), alpha[t], stat)
        for s in range(num_tasks):
            stat = jnp.where(jnp.logical_and(tile_rows == 1 + t, lanes == s), entry[t, s], stat)
    stat_ref[...] = stat

    wts = [a[0:1, 0:1] for a in alpha]

    for block in range(CHIPS):
        for layer in range(num_layers):
            gsend[block, layer] = (wts[0] * recvu[layer, 0, block] + wts[1] * recvu[layer, 1, block]
                                   + wts[2] * recvu[layer, 2, block])
    g_copies = []
    for slot in range(3):
        g_copies.append(pltpu.make_async_remote_copy(
            src_ref=gsend.at[peer_chip[slot]], dst_ref=grecv.at[slot], send_sem=gs_sem.at[slot],
            recv_sem=gr_sem.at[slot], device_id=(peers[slot],), device_id_type=MESH))
        g_copies[-1].start()

    def put_rows(out_ref, layer, rows, row0, row_tiles, col_tile, val):
        for piece in range(val.shape[1] // 128):
            start = row0 * row_tiles * num_layers + (col_tile + piece) * num_layers + layer
            out_ref[pl.ds(start, rows, stride=row_tiles * num_layers), :] = val[:, piece * 128:(piece + 1) * 128]

    @pl.loop(0, 4)
    def _(block):
        rows = pl.ds(pl.multiple_of(block * 48, 48), 48)
        for layer in range(num_layers):
            val = wts[0] * recvd[layer, 0, rows] + wts[1] * recvd[layer, 1, rows] + wts[2] * recvd[layer, 2, rows]
            put_rows(outd_ref, layer, 48, block * 48, dim // 128, 0, val)

    for layer in range(num_layers):
        put_rows(outu_ref, layer, 48, 0, ff // 128, chip * (ffq // 128), gsend[chip, layer])
    for slot in range(3):
        g_copies[slot].wait_recv()
        for layer in range(num_layers):
            put_rows(outu_ref, layer, 48, 0, ff // 128, peer_chip[slot] * (ffq // 128), grecv[slot, layer])
    for slot in range(3):
        g_copies[slot].wait_send()
    for copy in m_copies:
        copy.wait_send()


def solution(mesh):
    num_dev = mesh.shape['data']

    def local_step(x_local, lab_local, w_up, w_down, task_heads):
        num_layers, dim, ff = w_up.shape
        num_tasks = task_heads.shape[0]
        tok = x_local.shape[0]
        ffq = ff // CHIPS
        inv_tokens = 1.0 / (tok * num_dev)
        share = num_layers * dim * ff // num_dev // 128
        vmem = pl.BlockSpec(memory_space=pltpu.VMEM)
        hbm = pl.BlockSpec(memory_space=pl.ANY)

        def body(*refs):
            trunk_kernel(inv_tokens, *refs)

        dma = pltpu.SemaphoreType.DMA
        stat, out_up, out_down = pl.pallas_call(
            body,
            out_shape=(jax.ShapeDtypeStruct((8, 128), F32), jax.ShapeDtypeStruct((share, 128), F32),
                       jax.ShapeDtypeStruct((share, 128), F32)),
            in_specs=[vmem, vmem, hbm, hbm, vmem],
            out_specs=(vmem, vmem, vmem),
            scratch_shapes=[
                pltpu.VMEM((num_layers, dim, ff), BF16),
                pltpu.VMEM((num_layers, ff, dim), BF16),
                pltpu.VMEM((3, tok, dim), BF16),
                pltpu.VMEM((3, num_tasks, tok), jnp.int32),
                pltpu.VMEM((num_layers + 1, tok, dim), BF16),
                pltpu.VMEM((num_layers, tok, ff), F32),
                pltpu.VMEM((tok, ff), BF16),
                pltpu.VMEM((num_layers, tok, ffq), BF16),
                pltpu.VMEM((num_tasks, tok, dim), BF16),
                pltpu.VMEM((tok, num_tasks * dim), BF16),
                pltpu.VMEM((num_tasks, tok, ff), BF16),
                pltpu.VMEM((tok, num_tasks * ffq), BF16),
                pltpu.VMEM((num_layers, num_tasks, CHIPS, CORES, dim // num_dev, ffq), F32),
                pltpu.VMEM((num_layers, num_tasks, CORES, ffq // CORES, dim), F32),
                pltpu.VMEM((num_layers, num_tasks, CHIPS, dim // num_dev, ffq), F32),
                pltpu.VMEM((num_layers, num_tasks, ffq // CORES, dim), F32),
                pltpu.VMEM((CHIPS, num_layers, dim // num_dev, ffq), F32),
                pltpu.VMEM((3, num_layers, dim // num_dev, ffq), F32),
                pltpu.VMEM((num_dev, 8, 128), F32),
                dma((2, num_layers)), dma((3,)), dma((3,)), dma((3,)), dma((3,)),
                dma((num_layers,)), dma((num_layers,)), dma((num_layers,)), dma((num_layers,)),
                dma((num_dev - 1,)), dma((num_dev - 1,)), dma((3,)), dma((3,)),
            ],
            compiler_params=pltpu.CompilerParams(
                collective_id=0, has_side_effects=True, vmem_limit_bytes=67043328),
        )(x_local, lab_local, w_up, w_down, task_heads)

        def unpack(packed):
            tiles = packed.reshape(share // num_layers, num_layers, 128)
            return jnp.transpose(tiles, (1, 0, 2)).reshape(num_layers, -1)

        return stat[0, :num_tasks], stat[1:1 + num_tasks, :num_tasks], unpack(out_up), unpack(out_down)

    return jax.shard_map(local_step, mesh=mesh, in_specs=(P('data', None), P(None, 'data'), P(), P(), P()),
                         out_specs=(P(), P(), P(None, 'data'), P(None, 'data')), check_vma=False)
```

time: 629 us -> 185 us (0.29); the launches traced: 617 us -> 185 us
  Pallas kernels: 0 us -> 176 us
  waiting for transfers between devices: 163 us -> 0 us
  matrix products: 152 us -> 0 us
  local copies, waits for them, and re-layouts: 156 us -> 7.6 us
  other arithmetic: 91.8 us -> 0 us
  starting transfers between devices: 29.4 us -> 0 us
  blocking collectives: 22.5 us -> 0 us
    pallas_call x0 -> x1, Pallas kernels: none -> 176 us  [local_step(): pl.pallas_call(body, out_shape=(jax.ShapeDtypeStruct((8, 128), F32), jax....]
    all_to_all x8 -> x0, waiting for transfers between devices: 163 us -> none  [scatter_sum(): received = lax.all_to_all(flat_part, 'data', 1, 0, tiled=True)]
    dot_general x31 -> x0, matrix products: 152 us -> none  [the longest x8 44.7 us: local_step(): jnp.einsum('ts,us->tu', grad_shard, grad_shard, precision=lax.Precision.H...]
    convert_element_type x24 -> x0, local copies, waits for them, and re-layouts: 150 us -> none  [scatter_sum(): (part_grad.reshape(num_tasks, -1) * inv_tokens).astype(jnp.bfloat16)]
    reduce_sum x49 -> x0, other arithmetic: 76.4 us -> none  [the longest x8 38.5 us: scatter_sum(): return jnp.sum(received, axis=0, dtype=jnp.float32)]
    all_to_all x8 -> x0, starting transfers between devices: 29.4 us -> none  [scatter_sum(): received = lax.all_to_all(flat_part, 'data', 1, 0, tiled=True)]
    psum x1 -> x0, blocking collectives: 22.5 us -> none  [local_step(): gram_mat = lax.psum(gram_part, 'data')]
    div x20 -> x0, other arithmetic: 12.1 us -> none  [simplex_weights(): alpha_vec = alpha_vec / jnp.sum(alpha_vec)]
  transfers between devices with their start and end apart: 8 -> 0, of which waited for: 8 -> 0; matrix products, arithmetic and copies ran while one was open for 44% -> 0% of each run, Pallas kernels for 0% -> 0%
where the time goes in v1:
time: 185 us
  Pallas kernels  176 us (95%)
  local copies, waits for them, and re-layouts  7.6 us (4%)
    pallas_call x1, Pallas kernels, local_step(): pl.pallas_call(body, out_shape=(jax.ShapeDtypeStruct((8, 128), F32), jax....  176 us
    unnamed x5, local copies, waits for them, and re-layouts  5.15 us

profile of v1, /device:TPU:0, one launch (start us, length us, event | category | flops | bytes accessed | tf_op | source)
XLA Modules:
  0.0 184.6 jit_solution(12100835759341031204)
XLA Ops:
  0.6 1.7 copy.9.refs_4_
  2.3 176.3 %shard_map.84 = (f32[8,128]{1,0:T(8,128)}, f32[2304,128]{1,0:T(8,128)}, f32[2304,128]{1,0:T(8,128)}) custom-call(bf16[512,384]{1,0:T(8,128)(2,1)} %refs_0_.1, s32[3,512]{1,0:T(4,128)} %refs_1_.1, bf16[4,384,1536]{2,1,0:T(8,128)(2,1)} %refs_2_.1, bf16[4,1536,384]{2,1,0:T(8,128)(2,1)} %refs_3_.1, bf16[3,384,13]{2,1,0:T(8,128)(2,1)} %copy.9.refs_4_), custom_call_target="tpu_custom_call" | custom-call | tf_op jit(solution)/shard_map/pallas_call | solution.py:359
  178.7 1.3 slice.7
  179.9 1.2 slice_bitcast_fusion
  181.1 0.0 copy-start
  181.1 2.5 %copy.14 = f32[4,73728]{1,0:T(4,128)} copy(f32[4,73728]{1,0:T(4,128)} %bitcast.13) | data formatting | bytes 2359296
  183.6 0.0 copy-done
  183.6 1.0 copy.15
Async XLA Ops:
  181.1 2.5 %copy-start = (f32[2304,128]{1,0:T(8,128)S(1)}, f32[2304,128]{1,0:T(8,128)}, u32[]{:S(2)}) copy-start(f32[2304,128]{1,0:T(8,128)} %get-tuple-element.9) | copy-start | bytes 3538948

commit v2 on v1

v2 whole, which is shorter than its diff:
```python
import math

import jax
import jax.numpy as jnp
from jax import lax
from jax.experimental import pallas as pl
from jax.experimental.pallas import tpu as pltpu
from jax.sharding import PartitionSpec as P

EG_STEPS = 20
MESH = pl.DeviceIdType.MESH
GELU_C = math.sqrt(2.0 / math.pi)
GELU_A = 0.044715
F32 = jnp.float32
BF16 = jnp.bfloat16
PAIRS = ((0, 0), (0, 1), (0, 2), (1, 1), (1, 2), (2, 2))
CORES = 2
CHIPS = 4
UNROLL = True


def dot_nn(lhs, rhs):
    return lax.dot_general(lhs, rhs, (((1,), (0,)), ((), ())), preferred_element_type=F32)


def dot_nt(lhs, rhs):
    return lax.dot_general(lhs, rhs, (((1,), (1,)), ((), ())), preferred_element_type=F32)


def dot_tn(lhs, rhs):
    return lax.dot_general(lhs, rhs, (((0,), (0,)), ((), ())), preferred_element_type=F32)


def dot_tt(lhs, rhs):
    return lax.dot_general(lhs, rhs, (((0,), (1,)), ((), ())), preferred_element_type=F32)


def gelu_act(pre):
    tanh_val = jnp.tanh(pre * (GELU_C + (GELU_C * GELU_A) * (pre * pre)))
    return pre * (0.5 * tanh_val + 0.5)


def gelu_slope(pre):
    sq_pre = pre * pre
    tanh_val = jnp.tanh(pre * (GELU_C + (GELU_C * GELU_A) * sq_pre))
    rise = pre * (0.5 * GELU_C + (1.5 * GELU_C * GELU_A) * sq_pre)
    return (0.5 * tanh_val + 0.5) + rise * (1.0 - tanh_val * tanh_val)


def trunk_kernel(inv_tokens, x_ref, lab_ref, w1_hbm, w2_hbm, head_ref, stat_ref, outu_ref, outd_ref,
                 w1, w2, xg, lg, hs, pre, akeep, afk, dcat, dsend, drecv, sbuf, scat, acc, mtile,
                 w_sem, xs_sem, xr_sem, ls_sem, lr_sem, es_sem, er_sem, ps_sem, pr_sem,
                 ms_sem, mr_sem, gs_sem, gr_sem, free_sem):
    num_layers, num_tasks = w1.shape[0], head_ref.shape[0]
    tok, dim = x_ref.shape
    ff = w1.shape[2]
    ffq = ff // CHIPS
    half = dim // CORES
    rows48 = dim // (CORES * CHIPS)
    num_dev = CORES * CHIPS
    me = lax.axis_index('data')
    chip, core = me // CORES, me % CORES
    mate = me + 1 - 2 * core
    mcore = 1 - core
    cx, cy = chip % 2, chip // 2
    peer_chip = (cy * 2 + (1 - cx), (1 - cy) * 2 + cx, (1 - cy) * 2 + (1 - cx))
    peers = tuple(pc * CORES + core for pc in peer_chip)

    w_copies = []
    for layer in range(num_layers):
        c1 = pltpu.make_async_copy(w1_hbm.at[layer], w1.at[layer], w_sem.at[0, layer])
        c2 = pltpu.make_async_copy(w2_hbm.at[layer], w2.at[layer], w_sem.at[1, layer])
        c1.start()
        c2.start()
        w_copies.append((c1, c2))

    barrier = pltpu.get_barrier_semaphore()
    for step in range(1, num_dev):
        pl.semaphore_signal(barrier, inc=1, device_id=(lax.rem(me + step, num_dev),), device_id_type=MESH)
    pl.semaphore_wait(barrier, num_dev - 1)

    def remote(src, dst, send, recv, dev):
        return pltpu.make_async_remote_copy(src_ref=src, dst_ref=dst, send_sem=send, recv_sem=recv,
                                            device_id=(dev,), device_id_type=MESH)

    x_copies = [remote(x_ref, xg.at[s], xs_sem.at[s], xr_sem.at[s], peers[s]) for s in range(3)]
    l_copies = [remote(lab_ref, lg.at[s], ls_sem.at[s], lr_sem.at[s], peers[s]) for s in range(3)]
    e_copies = [[remote(dsend.at[v], drecv.at[s, v], es_sem.at[s, v], er_sem.at[s, v], peers[s])
                 for v in range(num_layers - 1)] for s in range(2)]
    p_copies = [remote(acc.at[v, :, mcore], pre.at[pl.ds(v * num_tasks, num_tasks), pl.ds(0, dim)],
                       ps_sem.at[v], pr_sem.at[v], mate) for v in range(num_layers)]
    for slot in (2, 0, 1):
        x_copies[slot].start()
        l_copies[slot].start()

    fk = pl.ds(pl.multiple_of(chip * ffq, 128), ffq)

    def wide_blocks(body):
        if UNROLL:
            for blk in range(2):
                body(blk)
        else:
            @pl.loop(0, 2)
            def _(blk):
                body(blk)

    def wide_cols(blk):
        return pl.ds(pl.multiple_of(blk * 2 * ffq, 128), 2 * ffq)

    def forward(layer, keep):
        h_in = hs[layer]

        def body(blk):
            p_val = dot_nn(h_in, w1[layer, :, wide_cols(blk)])
            if keep:
                pre[(layer - 1) * CHIPS + 2 * blk] = p_val[:, :ffq]
                pre[(layer - 1) * CHIPS + 2 * blk + 1] = p_val[:, ffq:]
            sbuf[0, :, wide_cols(blk)] = gelu_act(p_val).astype(BF16)

        wide_blocks(body)
        if keep:
            akeep[layer - 1] = sbuf[0, :, fk]
        hs[layer + 1] = (h_in.astype(F32) + dot_nn(sbuf[0], w2[layer])).astype(BF16)

    def add_down(layer, a_val, d_val):
        down = dot_tn(a_val, d_val)
        for task in range(num_tasks):
            for par in range(CORES):
                acc[layer, task, par, half:] += down[par * half:(par + 1) * half, task * dim:(task + 1) * dim]

    def add_up(layer, h_val):
        up = dot_tn(h_val, scat[...])
        for task in range(num_tasks):
            for par in range(CORES):
                for blk in range(CHIPS):
                    row = (blk * CORES + par) * rows48
                    acc[layer, task, par, blk * rows48:(blk + 1) * rows48] += (
                        up[row:row + rows48, task * ffq:(task + 1) * ffq])

    def backward_full(layer):
        def body(blk):
            w_blk = w2[layer, wide_cols(blk), :]
            slopes = [gelu_slope(pre[(layer - 1) * CHIPS + 2 * blk + i]) for i in range(2)]
            for task in range(num_tasks):
                d_act = dot_nt(dcat[:, task * dim:(task + 1) * dim], w_blk)
                for i in range(2):
                    cols = pl.ds(pl.multiple_of((2 * blk + i) * ffq, 128), ffq)
                    sbuf[task, :, cols] = (d_act[:, i * ffq:(i + 1) * ffq] * slopes[i]).astype(BF16)

        wide_blocks(body)
        for task in range(num_tasks):
            scat[:, task * ffq:(task + 1) * ffq] = sbuf[task, :, fk]
        add_down(layer, akeep[layer - 1], dcat[...])
        for task in range(num_tasks):
            cols = slice(task * dim, (task + 1) * dim)
            dcat[:, cols] = (dcat[:, cols].astype(F32) + dot_nt(sbuf[task], w1[layer])).astype(BF16)
        add_up(layer, hs[layer])

    def backward_part(layer, h_val, d_ref):
        p_val = dot_nn(h_val, w1[layer, :, fk])
        slope = gelu_slope(p_val)
        afk[...] = gelu_act(p_val).astype(BF16)
        for task in range(num_tasks):
            d_act = dot_nt(d_ref[:, task * dim:(task + 1) * dim], w2[layer, fk, :])
            scat[:, task * ffq:(task + 1) * ffq] = (d_act * slope).astype(BF16)
        add_down(layer, afk[...], d_ref[...])
        add_up(layer, h_val)

    def head_errors(labels):
        z_val = hs[num_layers]
        for task in range(num_tasks):
            logits = dot_nt(head_ref[task], z_val)
            shifted = jnp.exp(logits - jnp.max(logits, axis=0, keepdims=True))
            probs = shifted / jnp.sum(shifted, axis=0, keepdims=True)
            rows = lax.broadcasted_iota(jnp.int32, probs.shape, 0)
            onehot = (rows == labels[task:task + 1, :]).astype(F32)
            err = (probs - onehot).astype(BF16)
            dcat[:, task * dim:(task + 1) * dim] = dot_tn(err, head_ref[task]).astype(BF16)

    @pl.loop(0, num_layers)
    def _(layer):
        acc[layer] = jnp.zeros(acc.shape[1:], F32)

    @pl.loop(0, 2)
    def _(turn):
        @pl.when(turn == 0)
        def _():
            hs[0] = x_ref[...]
            w_copies[0][0].wait()
            w_copies[0][1].wait()

        @pl.when(turn == 1)
        def _():
            x_copies[2].wait_recv()
            l_copies[2].wait_recv()
            hs[0] = xg[2]

        forward(0, False)

        @pl.loop(1, num_layers)
        def _(layer):
            for late in range(1, num_layers):
                @pl.when(jnp.logical_and(turn == 0, layer == late))
                def _():
                    w_copies[late][0].wait()
                    w_copies[late][1].wait()
            forward(layer, True)

        @pl.when(turn == 0)
        def _():
            head_errors(lab_ref[...])

        @pl.when(turn == 1)
        def _():
            head_errors(lg[2])

        @pl.loop(0, num_layers - 1)
        def _(back):
            layer = num_layers - 1 - back
            backward_full(layer)
            for lower in range(num_layers - 1):
                @pl.when(jnp.logical_and(turn == 0, layer == lower + 1))
                def _():
                    dsend[lower] = dcat[...]
                    e_copies[0][lower].start()
                    e_copies[1][lower].start()

        backward_part(0, hs[0], dcat)

    pl.semaphore_signal(free_sem, inc=1, device_id=(mate,), device_id_type=MESH)

    @pl.loop(0, 2)
    def _(slot):
        for side in range(2):
            @pl.when(slot == side)
            def _():
                x_copies[side].wait_recv()
                l_copies[side].wait_recv()
        hs[0] = xg[slot]

        @pl.loop(0, num_layers)
        def _(layer):
            forward(layer, False)

        head_errors(lg[slot])
        backward_part(num_layers - 1, hs[num_layers - 1], dcat)

        @pl.when(slot == 1)
        def _():
            pl.semaphore_wait(free_sem, 1)
            p_copies[num_layers - 1].start()

        @pl.loop(0, num_layers - 2)
        def _(back):
            layer = num_layers - 2 - back
            for side in range(2):
                for lower in range(1, num_layers - 1):
                    @pl.when(jnp.logical_and(slot == side, layer == lower))
                    def _():
                        e_copies[side][lower].wait_recv()
            backward_part(layer, hs[layer], drecv.at[slot, layer])
            for lower in range(1, num_layers - 1):
                @pl.when(jnp.logical_and(slot == 1, layer == lower))
                def _():
                    p_copies[lower].start()

    @pl.loop(0, 2)
    def _(slot):
        for side in range(2):
            @pl.when(slot == side)
            def _():
                e_copies[side][0].wait_recv()
        backward_part(0, xg[slot], drecv.at[slot, 0])

    p_copies[0].start()
    for slot in range(3):
        x_copies[slot].wait_send()
        l_copies[slot].wait_send()
    for side in range(2):
        for lower in range(num_layers - 1):
            e_copies[side][lower].wait_send()

    sums = tuple(jnp.zeros((8, 128), F32) for _ in PAIRS)

    def fold(val):
        part = jnp.sum(val.reshape(-1, 8, val.shape[-1]), axis=0)
        out = part[:, :128]
        for piece in range(1, part.shape[-1] // 128):
            out = out + part[:, piece * 128:(piece + 1) * 128]
        return out

    for layer in range(num_layers - 1, -1, -1):
        p_copies[layer].wait_recv()

        @pl.loop(0, dim // rows48, init_carry=sums)
        def sums(block, carry):
            rows = pl.ds(pl.multiple_of(block * rows48, 8), rows48)
            grads = []
            for task in range(num_tasks):
                val = (acc[layer, task, core, rows] + pre[layer * num_tasks + task, rows]) * inv_tokens
                pre[layer * num_tasks + task, rows] = val
                grads.append(val)
            return tuple(old + fold(grads[t] * grads[s]) for old, (t, s) in zip(carry, PAIRS))

    for layer in range(num_layers):
        p_copies[layer].wait_send()
    tile_rows = lax.broadcasted_iota(jnp.int32, (8, 128), 0)
    my_tile = jnp.zeros((8, 128), F32)
    for row, val in enumerate(sums):
        my_tile = jnp.where(tile_rows == row, jnp.sum(val, axis=0, keepdims=True), my_tile)
    mtile[me] = my_tile
    m_copies = []
    for step in range(1, num_dev):
        m_copies.append(remote(mtile.at[me], mtile.at[me], ms_sem.at[step - 1], mr_sem.at[step - 1],
                               lax.rem(me + step, num_dev)))
        m_copies[-1].start()
    for step in range(1, num_dev):
        from_dev = lax.rem(me + num_dev - step, num_dev)
        remote(mtile.at[from_dev], mtile.at[from_dev], ms_sem.at[step - 1], mr_sem.at[step - 1],
               lax.rem(me + step, num_dev)).wait_recv()
    total = mtile[0]
    for dev in range(1, num_dev):
        total = total + mtile[dev]
    total = jnp.broadcast_to(jnp.sum(total, axis=1, keepdims=True), (8, 128))
    entry = {}
    for row, (t, s) in enumerate(PAIRS):
        val = jnp.broadcast_to(total[row:row + 1, :], (8, 128))
        entry[t, s] = val
        entry[s, t] = val
    tau = (entry[0, 0] + entry[1, 1] + entry[2, 2]) / num_tasks
    alpha = [jnp.full((8, 128), 1.0 / num_tasks, F32) for _ in range(num_tasks)]
    for step in range(EG_STEPS):
        pulls = [entry[t, 0] * alpha[0] + entry[t, 1] * alpha[1] + entry[t, 2] * alpha[2] for t in range(num_tasks)]
        alpha = [alpha[t] * jnp.exp(-pulls[t] / tau) for t in range(num_tasks)]
        norm = alpha[0] + alpha[1] + alpha[2]
        alpha = [a / norm for a in alpha]
    wts = [a[0:1, 0:1] for a in alpha]

    def mix(layer, rows):
        out = wts[0] * pre[layer * num_tasks, rows]
        for task in range(1, num_tasks):
            out = out + wts[task] * pre[layer * num_tasks + task, rows]
        return out

    for blk in range(CHIPS):
        rows = slice(blk * rows48, (blk + 1) * rows48)
        for layer in range(num_layers):
            acc[layer, 0, mcore, rows] = mix(layer, rows)
    g_copies = []
    for slot in range(3):
        g_src = acc.at[:, 0, mcore, pl.ds(pl.multiple_of(peer_chip[slot] * rows48, 8), rows48)]
        g_dst = acc.at[:, 1, mcore, pl.ds(slot * rows48, rows48)]
        g_copies.append(remote(g_src, g_dst, gs_sem.at[slot], gr_sem.at[slot], peers[slot]))
    for slot in (2, 0, 1):
        g_copies[slot].start()

    lanes = lax.broadcasted_iota(jnp.int32, (8, 128), 1)
    stat = jnp.zeros((8, 128), F32)
    for t in range(num_tasks):
        stat = jnp.where(jnp.logical_and(tile_rows == 0, lanes == t), alpha[t], stat)
        for s in range(num_tasks):
            stat = jnp.where(jnp.logical_and(tile_rows == 1 + t, lanes == s), entry[t, s], stat)
    stat_ref[...] = stat

    def put_rows(out_ref, layer, row0, row_tiles, col_tile, val):
        for piece in range(val.shape[1] // 128):
            start = row0 * row_tiles * num_layers + (col_tile + piece) * num_layers + layer
            out_ref[pl.ds(start, val.shape[0], stride=row_tiles * num_layers), :] = val[:, piece * 128:(piece + 1) * 128]

    @pl.loop(0, CHIPS)
    def _(block):
        rows = pl.ds(pl.multiple_of(half + block * rows48, 8), rows48)
        for layer in range(num_layers):
            put_rows(outd_ref, layer, block * rows48, dim // 128, 0, mix(layer, rows))

    own_rows = pl.ds(pl.multiple_of(chip * rows48, 8), rows48)
    for layer in range(num_layers):
        put_rows(outu_ref, layer, 0, ff // 128, chip * (ffq // 128), acc[layer, 0, mcore, own_rows])
    for slot in range(3):
        g_copies[slot].wait_recv()
        for layer in range(num_layers):
            put_rows(outu_ref, layer, 0, ff // 128, peer_chip[slot] * (ffq // 128),
                     acc[layer, 1, mcore, slot * rows48:(slot + 1) * rows48])
    for slot in range(3):
        g_copies[slot].wait_send()
    for copy in m_copies:
        copy.wait_send()


def solution(mesh):
    num_dev = mesh.shape['data']

    def local_step(x_local, lab_local, w_up, w_down, task_heads):
        num_layers, dim, ff = w_up.shape
        num_tasks = task_heads.shape[0]
        tok = x_local.shape[0]
        ffq = ff // CHIPS
        inv_tokens = 1.0 / (tok * num_dev)
        share = num_layers * dim * ff // num_dev // 128
        vmem = pl.BlockSpec(memory_space=pltpu.VMEM)
        hbm = pl.BlockSpec(memory_space=pl.ANY)

        def body(*refs):
            trunk_kernel(inv_tokens, *refs)

        dma = pltpu.SemaphoreType.DMA
        stat, out_up, out_down = pl.pallas_call(
            body,
            out_shape=(jax.ShapeDtypeStruct((8, 128), F32), jax.ShapeDtypeStruct((share, 128), F32),
                       jax.ShapeDtypeStruct((share, 128), F32)),
            in_specs=[vmem, vmem, hbm, hbm, vmem],
            out_specs=(vmem, vmem, vmem),
            scratch_shapes=[
                pltpu.VMEM((num_layers, dim, ff), BF16),
                pltpu.VMEM((num_layers, ff, dim), BF16),
                pltpu.VMEM((3, tok, dim), BF16),
                pltpu.VMEM((3, num_tasks, tok), jnp.int32),
                pltpu.VMEM((num_layers + 1, tok, dim), BF16),
                pltpu.VMEM(((num_layers - 1) * CHIPS, tok, ffq), F32),
                pltpu.VMEM((num_layers - 1, tok, ffq), BF16),
                pltpu.VMEM((tok, ffq), BF16),
                pltpu.VMEM((tok, num_tasks * dim), BF16),
                pltpu.VMEM((num_layers - 1, tok, num_tasks * dim), BF16),
                pltpu.VMEM((2, num_layers - 1, tok, num_tasks * dim), BF16),
                pltpu.VMEM((num_tasks, tok, ff), BF16),
                pltpu.VMEM((tok, num_tasks * ffq), BF16),
                pltpu.VMEM((num_layers, num_tasks, CORES, 2 * (dim // CORES), ffq), F32),
                pltpu.VMEM((num_dev, 8, 128), F32),
                dma((2, num_layers)), dma((3,)), dma((3,)), dma((3,)), dma((3,)),
                dma((2, num_layers - 1)), dma((2, num_layers - 1)), dma((num_layers,)), dma((num_layers,)),
                dma((num_dev - 1,)), dma((num_dev - 1,)), dma((3,)), dma((3,)), pltpu.SemaphoreType.REGULAR,
            ],
            compiler_params=pltpu.CompilerParams(
                collective_id=0, has_side_effects=True, vmem_limit_bytes=67043328),
        )(x_local, lab_local, w_up, w_down, jnp.transpose(task_heads, (0, 2, 1)))

        def unpack(packed):
            tiles = packed.reshape(share // num_layers, num_layers, 128)
            return jnp.transpose(tiles, (1, 0, 2)).reshape(num_layers, -1)

        return stat[0, :num_tasks], stat[1:1 + num_tasks, :num_tasks], unpack(out_up), unpack(out_down)

    return jax.shard_map(local_step, mesh=mesh, in_specs=(P('data', None), P(None, 'data'), P(), P(), P()),
                         out_specs=(P(), P(), P(None, 'data'), P(None, 'data')), check_vma=False)
```

time: 185 us -> 142 us (0.77)
  Pallas kernels: 176 us -> 135 us
    pallas_call x1, Pallas kernels: 176 us -> 135 us  [local_step(): pl.pallas_call(body, out_shape=(jax.ShapeDtypeStruct((8, 128), F32), jax....]
    unnamed x5 -> x4, local copies, waits for them, and re-layouts: 5.15 us -> 3.47 us
where the time goes in v2:
time: 142 us
  Pallas kernels  135 us (95%)
  local copies, waits for them, and re-layouts  5.92 us (4%)
    pallas_call x1, Pallas kernels, local_step(): pl.pallas_call(body, out_shape=(jax.ShapeDtypeStruct((8, 128), F32), jax....  135 us
    unnamed x4, local copies, waits for them, and re-layouts  3.47 us

profile of v2, /device:TPU:0, one launch (start us, length us, event | category | flops | bytes accessed | tf_op | source)
XLA Modules:
  0.0 141.7 jit_solution(8703216475936176041)
XLA Ops:
  0.6 135.2 %shard_map.84 = (f32[8,128]{1,0:T(8,128)}, f32[2304,128]{1,0:T(8,128)}, f32[2304,128]{1,0:T(8,128)}) custom-call(bf16[512,384]{1,0:T(8,128)(2,1)} %refs_0_.1, s32[3,512]{1,0:T(4,128)} %refs_1_.1, bf16[4,384,1536]{2,1,0:T(8,128)(2,1)} %refs_2_.1, bf16[4,1536,384]{2,1,0:T(8,128)(2,1)} %refs_3_.1, bf16[3,13,384]{2,1,0:T(8,128)(2,1)} %bitcast.15), custom_call_target="tpu_custom_call" | custom-call | tf_op jit(solution)/shard_map/pallas_call | solution.py:407
  135.8 1.3 slice.7
  137.1 1.2 slice_bitcast_fusion
  138.3 0.0 copy-start
  138.3 2.5 %copy.13 = f32[4,73728]{1,0:T(4,128)} copy(f32[4,73728]{1,0:T(4,128)} %bitcast.14) | data formatting | bytes 2359296
  140.7 0.0 copy-done
  140.7 1.0 copy.14
Async XLA Ops:
  138.3 2.5 %copy-start = (f32[2304,128]{1,0:T(8,128)S(1)}, f32[2304,128]{1,0:T(8,128)}, u32[]{:S(2)}) copy-start(f32[2304,128]{1,0:T(8,128)} %get-tuple-element.9) | copy-start | bytes 3538948
